TPU v7x, 32 devices: a whole 2x2x4 slice. The times are simulated.
32 devices in a mesh: blk: 8 (over z, x), dp: 4 (over y, core).
Axes of the slice: x: 2, y: 2, z: 4, core: 2. Of those that a mesh axis runs over, the one named last changes fastest.
Arguments:
- embeddings: bfloat16 [8192, 512], P(('dp', 'blk')), may hold values from -16 to 16
- centers: bfloat16 [16384, 512], P(('blk', 'dp')), may hold values from -10 to 10
- labels: int32 [8192], P(('dp', 'blk')), may hold values from 0 to 16383
Outputs:
- loss: float32 [8192], P(('dp', 'blk'))
All inputs are finite; a program needn't handle non-finite values.
Results may differ from a plain program's by a relative error of at most 0.0017.
Values may be sent and summed in bfloat16 or wider, within the bound.
A program may use at most 128 MiB of HBM per device.

v0:
```python
import math
import jax
import jax.numpy as jnp
from jax import lax
from jax.sharding import PartitionSpec as P

EPSILON = 1e-06
LOGIT_SCALE = 30.0
MARGIN = 0.5


def unit_rows(matrix):
    values = matrix.astype(jnp.float32)
    return (values * lax.rsqrt(jnp.sum(values * values, axis=1, keepdims=True) + EPSILON)).astype(
        jnp.bfloat16
    )


def margin_loss(other_sum, target_cos):
    sine = jnp.sqrt(jnp.maximum(1.0 - target_cos * target_cos, 0.0))
    shifted = target_cos * math.cos(MARGIN) - sine * math.sin(MARGIN)
    return (
        LOGIT_SCALE
        + jnp.log(other_sum + jnp.exp(LOGIT_SCALE * shifted - LOGIT_SCALE))
        - LOGIT_SCALE * shifted
    )


def block_terms(rows, row_labels, centers_block, class_start):
    cosine = jnp.einsum("nd,cd->nc", rows, centers_block, preferred_element_type=jnp.float32)
    columns = class_start + jnp.arange(centers_block.shape[0], dtype=jnp.int32)
    is_target = row_labels[:, None] == columns[None, :]
    other_sum = jnp.sum(
        jnp.where(is_target, 0.0, jnp.exp(LOGIT_SCALE * cosine - LOGIT_SCALE)), axis=1
    )
    target_cos = jnp.sum(jnp.where(is_target, cosine, 0.0), axis=1)
    return (other_sum, target_cos)


def body(embeddings, centers, labels):
    emb_unit = unit_rows(embeddings)
    center_unit = unit_rows(centers)
    shard_classes = center_unit.shape[0]
    group_count = lax.axis_size("dp")
    group_index = lax.axis_index("dp")
    group_rows, group_labels = (
        lax.all_gather(emb_unit, "dp", axis=0, tiled=True),
        lax.all_gather(labels, "dp", axis=0, tiled=True),
    )
    group_total = group_rows.shape[0]
    zeros_sum = jnp.zeros((group_total,), jnp.float32)
    pieces = lax.all_gather(center_unit, "blk", axis=0, tiled=True)
    span_rows = math.gcd(math.gcd(pieces.shape[0], shard_classes), 512)

    def one_span(accum, step_index):
        first = step_index * span_rows
        block_rows = lax.dynamic_slice_in_dim(pieces, step_index * span_rows, span_rows, 0)
        class_start = (
            first // shard_classes * group_count + group_index
        ) * shard_classes + first % shard_classes
        other_part, target_part = block_terms(group_rows, group_labels, block_rows, class_start)
        return ((accum[0] + other_part, accum[1] + target_part), None)

    result, ignored = lax.scan(
        one_span, (zeros_sum, zeros_sum), jnp.arange(pieces.shape[0] // span_rows, dtype=jnp.int32)
    )
    other_group, target_group = result
    other_sum, target_cos = (
        lax.psum_scatter(other_group, "dp", scatter_dimension=0, tiled=True),
        lax.psum_scatter(target_group, "dp", scatter_dimension=0, tiled=True),
    )
    return margin_loss(other_sum, target_cos)


def solution(mesh):
    return jax.shard_map(
        body,
        mesh=mesh,
        in_specs=(P(("dp", "blk"), None), P(("blk", "dp"), None), P(("dp", "blk"))),
        out_specs=P(("dp", "blk")),
        check_vma=False,
    )
```

profile of v0, /device:TPU:0, one launch (start us, length us, event | category | flops | bytes accessed | tf_op | source)
XLA Modules:
  0.0 147.6 jit_solution(2375820200223989825)
XLA Ops:
  6.5 1.1 fusion.9
  7.7 1.8 %fusion.10 = bf16[256,512]{1,0:T(8,128)(2,1)} fusion(bf16[256,512]{1,0:T(8,128)(2,1)} %param.5, f32[256]{0:T(256)S(1)} %add_rsqrt_fusion.1), kind=kLoop, calls=%fused_computation.20 | loop fusion | flops 393216 | bytes 525312 | tf_op jit(solution)/shard_map/convert_element_type | solution.py:14
  9.5 1.2 fusion.7
  10.7 2.0 %fusion.8 = bf16[512,512]{1,0:T(8,128)(2,1)} fusion(bf16[512,512]{1,0:T(8,128)(2,1)} %param.6, f32[512]{0:T(512)S(1)} %add_rsqrt_fusion), kind=kLoop, calls=%fused_computation.16 | loop fusion | flops 786432 | bytes 1050624 | tf_op jit(solution)/shard_map/convert_element_type | solution.py:14
  14.1 6.0 %all-gather = s32[4,1,256]{2,1,0:T(1,128)S(1)} all-gather(s32[1,1,256]{2,1,0:T(1,128)S(1)} %bitcast.21), channel_id=1, replica_groups=mesh['blk'=8,'dp'=4] {'dp'}, dimensions={0}, use_global_device_ids=true | all-gather | bytes 5120 | tf_op jit(solution)/shard_map/all_gather | solution.py:48
  20.1 8.9 %all-gather.6.cloned.1.call-done = bf16[1024,512]{1,0:T(8,128)(2,1)} async-done(((bf16[256,512]{1,0:T(8,128)(2,1)}), bf16[1024,512]{1,0:T(8,128)(2,1)}) %all-gather.6.cloned.1.call-update) | async-done | bytes 1048592 | tf_op jit(solution)/shard_map/all_gather | solution.py:47
  29.0 75.0 %all-gather.4.cloned.1.call-done = bf16[4096,512]{1,0:T(8,128)(2,1)} async-done(((bf16[512,512]{1,0:T(8,128)(2,1)}), bf16[4096,512]{1,0:T(8,128)(2,1)}) %all-gather.4.cloned.1.call-update) | async-done | bytes 4194320 | tf_op jit(solution)/shard_map/all_gather | solution.py:52
  104.0 30.3 %while.15 = (s32[]{:T(128)}, f32[1024]{0:T(1024)S(1)}, f32[1024]{0:T(1024)S(1)}, s32[1024]{0:T(1024)S(1)}, s32[8]{0:T(128)S(1)}, /*index=5*/s32[]{:T(128)}, bf16...) while((s32[]{:T(128)}, f32[1024]{0:T(1024)S(1)}, ...), condition=%wide.region_5.6_spmd.clone, body=%wide.region_2.5_spmd.clone.sunk | while | flops 540543488 | bytes 1614283 | solution.py:64
  105.3 2.4 %fusion.18 = (f32[1024]{0:T(1024)S(1)}, f32[1024]{0:T(1024)S(1)}) fusion(s32[1024]{0:T(1024)S(1)} %get-tuple-element.256, s32[512]{0:T(512)S(1)} %iota_add_fusion.2, bf16[1024,512]{1,0:T(8,128)(2,1)} %get-tuple-element.260, bf16[4096,512]{1,0:T(8,128)(2,1)} %get-tuple-element.259, s32[]{:T(128)S(6)} %select_n.57), kind=kOutput, calls=%fused_computation.3.clone.1 | convolution fusion | flops 540538880 | bytes 1587204 | tf_op jit(solution)/shard_map/while/body/eval_jaxpr/nd,cd->nc/dot_general | solution.py:30
  107.8 0.6 dynamic_slice.22
  109.1 2.4 %fusion.18 = (f32[1024]{0:T(1024)S(1)}, f32[1024]{0:T(1024)S(1)}) fusion(s32[1024]{0:T(1024)S(1)} %get-tuple-element.256, s32[512]{0:T(512)S(1)} %iota_add_fusion.2, bf16[1024,512]{1,0:T(8,128)(2,1)} %get-tuple-element.260, bf16[4096,512]{1,0:T(8,128)(2,1)} %get-tuple-element.259, s32[]{:T(128)S(6)} %select_n.57), kind=kOutput, calls=%fused_computation.3.clone.1 | convolution fusion | flops 540538880 | bytes 1587204 | tf_op jit(solution)/shard_map/while/body/eval_jaxpr/nd,cd->nc/dot_general | solution.py:30
  111.6 0.6 dynamic_slice.22
  112.9 2.4 %fusion.18 = (f32[1024]{0:T(1024)S(1)}, f32[1024]{0:T(1024)S(1)}) fusion(s32[1024]{0:T(1024)S(1)} %get-tuple-element.256, s32[512]{0:T(512)S(1)} %iota_add_fusion.2, bf16[1024,512]{1,0:T(8,128)(2,1)} %get-tuple-element.260, bf16[4096,512]{1,0:T(8,128)(2,1)} %get-tuple-element.259, s32[]{:T(128)S(6)} %select_n.57), kind=kOutput, calls=%fused_computation.3.clone.1 | convolution fusion | flops 540538880 | bytes 1587204 | tf_op jit(solution)/shard_map/while/body/eval_jaxpr/nd,cd->nc/dot_general | solution.py:30
  116.7 2.4 %fusion.18 = (f32[1024]{0:T(1024)S(1)}, f32[1024]{0:T(1024)S(1)}) fusion(s32[1024]{0:T(1024)S(1)} %get-tuple-element.256, s32[512]{0:T(512)S(1)} %iota_add_fusion.2, bf16[1024,512]{1,0:T(8,128)(2,1)} %get-tuple-element.260, bf16[4096,512]{1,0:T(8,128)(2,1)} %get-tuple-element.259, s32[]{:T(128)S(6)} %select_n.57), kind=kOutput, calls=%fused_computation.3.clone.1 | convolution fusion | flops 540538880 | bytes 1587204 | tf_op jit(solution)/shard_map/while/body/eval_jaxpr/nd,cd->nc/dot_general | solution.py:30
  119.2 0.6 dynamic_slice.22
  120.5 2.4 %fusion.18 = (f32[1024]{0:T(1024)S(1)}, f32[1024]{0:T(1024)S(1)}) fusion(s32[1024]{0:T(1024)S(1)} %get-tuple-element.256, s32[512]{0:T(512)S(1)} %iota_add_fusion.2, bf16[1024,512]{1,0:T(8,128)(2,1)} %get-tuple-element.260, bf16[4096,512]{1,0:T(8,128)(2,1)} %get-tuple-element.259, s32[]{:T(128)S(6)} %select_n.57), kind=kOutput, calls=%fused_computation.3.clone.1 | convolution fusion | flops 540538880 | bytes 1587204 | tf_op jit(solution)/shard_map/while/body/eval_jaxpr/nd,cd->nc/dot_general | solution.py:30
  123.0 0.6 dynamic_slice.22
  124.3 2.4 %fusion.18 = (f32[1024]{0:T(1024)S(1)}, f32[1024]{0:T(1024)S(1)}) fusion(s32[1024]{0:T(1024)S(1)} %get-tuple-element.256, s32[512]{0:T(512)S(1)} %iota_add_fusion.2, bf16[1024,512]{1,0:T(8,128)(2,1)} %get-tuple-element.260, bf16[4096,512]{1,0:T(8,128)(2,1)} %get-tuple-element.259, s32[]{:T(128)S(6)} %select_n.57), kind=kOutput, calls=%fused_computation.3.clone.1 | convolution fusion | flops 540538880 | bytes 1587204 | tf_op jit(solution)/shard_map/while/body/eval_jaxpr/nd,cd->nc/dot_general | solution.py:30
  126.8 0.6 dynamic_slice.22
  128.1 2.4 %fusion.18 = (f32[1024]{0:T(1024)S(1)}, f32[1024]{0:T(1024)S(1)}) fusion(s32[1024]{0:T(1024)S(1)} %get-tuple-element.256, s32[512]{0:T(512)S(1)} %iota_add_fusion.2, bf16[1024,512]{1,0:T(8,128)(2,1)} %get-tuple-element.260, bf16[4096,512]{1,0:T(8,128)(2,1)} %get-tuple-element.259, s32[]{:T(128)S(6)} %select_n.57), kind=kOutput, calls=%fused_computation.3.clone.1 | convolution fusion | flops 540538880 | bytes 1587204 | tf_op jit(solution)/shard_map/while/body/eval_jaxpr/nd,cd->nc/dot_general | solution.py:30
  130.5 0.6 dynamic_slice.22
  131.9 2.4 %fusion.18 = (f32[1024]{0:T(1024)S(1)}, f32[1024]{0:T(1024)S(1)}) fusion(s32[1024]{0:T(1024)S(1)} %get-tuple-element.256, s32[512]{0:T(512)S(1)} %iota_add_fusion.2, bf16[1024,512]{1,0:T(8,128)(2,1)} %get-tuple-element.260, bf16[4096,512]{1,0:T(8,128)(2,1)} %get-tuple-element.259, s32[]{:T(128)S(6)} %select_n.57), kind=kOutput, calls=%fused_computation.3.clone.1 | convolution fusion | flops 540538880 | bytes 1587204 | tf_op jit(solution)/shard_map/while/body/eval_jaxpr/nd,cd->nc/dot_general | solution.py:30
  134.3 5.8 %all-reduce.2 = (f32[1024]{0:T(1024)S(1)}, f32[1024]{0:T(1024)S(1)}) all-reduce(f32[1024]{0:T(1024)S(1)} %get-tuple-element.111, f32[1024]{0:T(1024)S(1)} %get-tuple-element.112), channel_id=2, replica_groups=mesh['blk'=8,'dp'=4] {'dp'}, use_global_device_ids=true, to_apply=%region_6.7.clone | all-reduce | flops 2048 | bytes 16384
  140.1 0.7 fusion.13
  (32 shorter events, 2.0 us)
Async XLA Ops:
  6.5 6.3 %copy-start.1 = (u32[32]{0:T(128)S(1)}, u32[32]{0:T(128)}, u32[]{:S(2)}) copy-start(u32[32]{0:T(128)} %constant.103) | copy-start | bytes 388
  6.5 7.5 %copy-start = (s32[256]{0:T(256)S(1)}, s32[256]{0:T(256)}, u32[]{:S(2)}) copy-start(s32[256]{0:T(256)} %param.7) | copy-start | bytes 3076
  6.5 22.5 %all-gather.6.cloned.1.call-start = ((), (), s32[]{:S(2)}) async-start(), calls=%async_computation.1 | async-start | bytes 1310720 | tf_op jit(solution)/shard_map/all_gather | solution.py:47
  9.5 94.5 %all-gather.4.cloned.1.call-start = ((), (), s32[]{:S(2)}) async-start(), calls=%async_computation | async-start | bytes 4718592 | tf_op jit(solution)/shard_map/all_gather | solution.py:52
Sparse Core Ops, SparseCore 0:
  9.6 19.4 all-gather.5
  31.2 72.7 all-gather.3
where the time goes:
time: 148 us
  waiting for transfers between devices  83.9 us (57%)
  matrix products  19.6 us (13%)
  between operations  14.1 us (10%)
  blocking collectives  11.8 us (8%)
  other arithmetic  6.88 us (5%)
  loops' own time  5.78 us (4%)
  local copies, waits for them, and re-layouts  5.52 us (4%)
    all_gather x1, waiting for transfers between devices, body(): pieces = lax.all_gather(center_unit, 'blk', axis=0, tiled=True)  75 us
    dot_general x8, matrix products, block_terms(): jnp.einsum('nd,cd->nc', rows, centers_block, preferred_element_type=jnp.f...  19.6 us
    all_gather x1, waiting for transfers between devices, body(): lax.all_gather(emb_unit, 'dp', axis=0, tiled=True)  8.92 us
    all_gather x1, blocking collectives, body(): lax.all_gather(labels, 'dp', axis=0, tiled=True)  6.04 us
    another operation x1, loops' own time, body(): lax.scan(one_span, (zeros_sum, zeros_sum), jnp.arange(pieces.shape[0] //...  5.78 us
    unnamed x1, blocking collectives  5.77 us
    dynamic_slice x8, local copies, waits for them, and re-layouts, body(): lax.scan(one_span, (zeros_sum, zeros_sum), jnp.arange(pieces.shape[0] //...  4.9 us
    convert_element_type x2, other arithmetic, unit_rows(): (values * lax.rsqrt(jnp.sum(values * values, axis=1, keepdims=True) + EPS...  3.79 us
  transfers between devices with their start and end apart: 2, of which 2 were waited for; matrix products, arithmetic and copies ran while one was open for 3% of the time, Pallas kernels for 0%

commit v1 on v0

--- a/solution.py
+++ b/solution.py
@@ -38,6 +38,19 @@
 
 
 def body(embeddings, centers, labels):
+
+    def edit_frames(a0, shard_axis):
+        num_devices = lax.axis_size(shard_axis)
+        inbox = list(map(lambda t: (t, (t + 1) % num_devices), range(num_devices)))
+
+        def load_bands(even):
+            if len(even) == num_devices:
+                return even
+            return load_bands([lax.ppermute(even[0], shard_axis, inbox), *even])
+
+        kept_arr = jnp.concatenate(load_bands([a0]), axis=0)
+        return jnp.roll(kept_arr, shift=(lax.axis_index(shard_axis) + 1) * a0.shape[0], axis=0)
+
     emb_unit = unit_rows(embeddings)
     center_unit = unit_rows(centers)
     shard_classes = center_unit.shape[0]
@@ -49,7 +62,7 @@
     )
     group_total = group_rows.shape[0]
     zeros_sum = jnp.zeros((group_total,), jnp.float32)
-    pieces = lax.all_gather(center_unit, "blk", axis=0, tiled=True)
+    pieces = edit_frames(center_unit, "blk")
     span_rows = math.gcd(math.gcd(pieces.shape[0], shard_classes), 512)
 
     def one_span(accum, step_index):

time: 148 us -> 163 us (1.10)
  local copies, waits for them, and re-layouts: 5.52 us -> 13.4 us
  waiting for transfers between devices: 83.9 us -> 88.3 us
  starting transfers between devices: 0.04 us -> 3.04 us
    ppermute x0 -> x7, waiting for transfers between devices: none -> 87.6 us  [load_bands(): return load_bands([lax.ppermute(even[0], shard_axis, inbox), *even])]
    all_gather x1 -> x0, waiting for transfers between devices: 75 us -> none  [body(): pieces = lax.all_gather(center_unit, 'blk', axis=0, tiled=True)]
    all_gather x1, waiting for transfers between devices: 8.92 us -> 0.7 us  [body(): lax.all_gather(emb_unit, 'dp', axis=0, tiled=True)]
    unnamed x5 -> x17, local copies, waits for them, and re-layouts: 0.62 us -> 5.93 us
    ppermute x0 -> x7, starting transfers between devices: none -> 3.04 us  [load_bands(): return load_bands([lax.ppermute(even[0], shard_axis, inbox), *even])]
    dynamic_slice x0 -> x1, local copies, waits for them, and re-layouts: none -> 2.22 us  [edit_frames(): jnp.roll(kept_arr, shift=(lax.axis_index(shard_axis) + 1) * a0.shape[0],...]
  transfers between devices with their start and end apart: 2 -> 8, of which waited for: 2 -> 8; matrix products, arithmetic and copies ran while one was open for 3% -> 7% of each run, Pallas kernels for 0% -> 0%
where the time goes in v1:
time: 163 us; the launch traced here: 162 us
  waiting for transfers between devices  88.3 us (54%)
  matrix products  19.6 us (12%)
  between operations  14.2 us (9%)
  local copies, waits for them, and re-layouts  13.4 us (8%)
  blocking collectives  11.3 us (7%)
  other arithmetic  6.46 us (4%)
  loops' own time  5.79 us (4%)
  starting transfers between devices  3.04 us (2%)
    ppermute x7, waiting for transfers between devices, load_bands(): return load_bands([lax.ppermute(even[0], shard_axis, inbox), *even])  87.6 us
    dot_general x8, matrix products, block_terms(): jnp.einsum('nd,cd->nc', rows, centers_block, preferred_element_type=jnp.f...  19.6 us
    unnamed x1, blocking collectives  6 us
    unnamed x17, local copies, waits for them, and re-layouts  5.93 us
    another operation x1, loops' own time, body(): lax.scan(one_span, (zeros_sum, zeros_sum), jnp.arange(pieces.shape[0] //...  5.79 us
    all_gather x1, blocking collectives, body(): lax.all_gather(labels, 'dp', axis=0, tiled=True)  5.28 us
    dynamic_slice x8, local copies, waits for them, and re-layouts, body(): lax.scan(one_span, (zeros_sum, zeros_sum), jnp.arange(pieces.shape[0] //...  5.22 us
  transfers between devices with their start and end apart: 8, of which 8 were waited for; matrix products, arithmetic and copies ran while one was open for 7% of the time, Pallas kernels for 0%

profile of v1, /device:TPU:0, one launch (start us, length us, event | category | flops | bytes accessed | tf_op | source)
XLA Modules:
  0.0 162.0 jit_solution(17804812616271669002)
XLA Ops:
  6.5 1.3 fusion.7
  7.8 1.2 fusion.8
  9.1 3.0 %collective-permute-start = (bf16[512,512]{1,0:T(8,128)(2,1)S(1)}, bf16[512,512]{1,0:T(8,128)(2,1)S(1)}, u32[]{:S(2)}, u32[]{:S(2)}) collective-permute-start(bf16[512,512]{1,0:T(8,128)(2,1)S(1)} %fusion.8), channel_id=1, source_target_pairs={{0,4},{4,8},{8,12},{12,16},{16,20},{20,24},{24,28},{28,0},{1,5},{5... | collective-permute-start | bytes 1572872 | tf_op jit(solution)/shard_map/ppermute | solution.py:49
  12.1 15.0 %collective-permute-done = bf16[512,512]{1,0:T(8,128)(2,1)S(1)} collective-permute-done((bf16[512,512]{1,0:T(8,128)(2,1)S(1)}, bf16[512,512]{1,0:T(8,128)(2,1)S(1)}, u32[]{:S(2)}, u32[]{:S(2)}) %collective-permute-start) | collective-permute-done | bytes 524320 | tf_op jit(solution)/shard_map/ppermute | solution.py:49
  27.0 15.8 %collective-permute-done.1 = bf16[512,512]{1,0:T(8,128)(2,1)S(1)} collective-permute-done((bf16[512,512]{1,0:T(8,128)(2,1)S(1)}, bf16[512,512]{1,0:T(8,128)(2,1)S(1)}, u32[]{:S(2)}, u32[]{:S(2)}) %collective-permute-start.1) | collective-permute-done | bytes 524320 | tf_op jit(solution)/shard_map/ppermute | solution.py:49
  42.8 14.9 %collective-permute-done.2 = bf16[512,512]{1,0:T(8,128)(2,1)S(1)} collective-permute-done((bf16[512,512]{1,0:T(8,128)(2,1)S(1)}, bf16[512,512]{1,0:T(8,128)(2,1)S(1)}, u32[]{:S(2)}, u32[]{:S(2)}) %collective-permute-start.2) | collective-permute-done | bytes 524320 | tf_op jit(solution)/shard_map/ppermute | solution.py:49
  57.8 14.1 %collective-permute-done.3 = bf16[512,512]{1,0:T(8,128)(2,1)S(1)} collective-permute-done((bf16[512,512]{1,0:T(8,128)(2,1)S(1)}, bf16[512,512]{1,0:T(8,128)(2,1)S(1)}, u32[]{:S(2)}, u32[]{:S(2)}) %collective-permute-start.3) | collective-permute-done | bytes 524320 | tf_op jit(solution)/shard_map/ppermute | solution.py:49
  71.8 13.2 %collective-permute-done.4 = bf16[512,512]{1,0:T(8,128)(2,1)S(1)} collective-permute-done((bf16[512,512]{1,0:T(8,128)(2,1)S(1)}, bf16[512,512]{1,0:T(8,128)(2,1)S(1)}, u32[]{:S(2)}, u32[]{:S(2)}) %collective-permute-start.4) | collective-permute-done | bytes 524320 | tf_op jit(solution)/shard_map/ppermute | solution.py:49
  85.0 12.5 %collective-permute-done.5 = bf16[512,512]{1,0:T(8,128)(2,1)} collective-permute-done((bf16[512,512]{1,0:T(8,128)(2,1)S(1)}, bf16[512,512]{1,0:T(8,128)(2,1)}, u32[]{:S(2)}, u32[]{:S(2)}) %collective-permute-start.5) | collective-permute-done | bytes 524320 | tf_op jit(solution)/shard_map/ppermute | solution.py:49
  98.6 1.8 %fusion.10 = bf16[256,512]{1,0:T(8,128)(2,1)} fusion(bf16[256,512]{1,0:T(8,128)(2,1)} %param.5, f32[256]{0:T(256)S(1)} %add_rsqrt_fusion.1), kind=kLoop, calls=%fused_computation.20 | loop fusion | flops 393216 | bytes 525312 | tf_op jit(solution)/shard_map/convert_element_type | solution.py:14
  100.5 1.2 dynamic-slice
  102.3 5.3 %all-gather = s32[4,1,256]{2,1,0:T(1,128)S(1)} all-gather(s32[1,1,256]{2,1,0:T(1,128)} %bitcast.21), channel_id=1, replica_groups=mesh['blk'=8,'dp'=4] {'dp'}, dimensions={0}, use_global_device_ids=true | all-gather | bytes 5120 | tf_op jit(solution)/shard_map/all_gather | solution.py:61
  107.5 2.2 %collective-permute-done.6 = bf16[512,512]{1,0:T(8,128)(2,1)} collective-permute-done((bf16[512,512]{1,0:T(8,128)(2,1)}, bf16[512,512]{1,0:T(8,128)(2,1)}, u32[]{:S(2)}, u32[]{:S(2)}) %collective-permute-start.6) | collective-permute-done | bytes 524320 | tf_op jit(solution)/shard_map/ppermute | solution.py:49
  114.8 2.2 %constant_dynamic-slice_fusion = bf16[4096,512]{1,0:T(8,128)(2,1)} fusion(bf16[8192,512]{1,0:T(8,128)(2,1)S(1)} %constant_dynamic-update-slice_fusion, s32[]{:T(128)S(6)} %select_n.52), kind=kLoop, calls=%fused_computation.43 | loop fusion | bytes 8388612 | tf_op jit(solution)/shard_map/jit(_roll_dynamic)/dynamic_slice | solution.py:52
  117.8 30.7 %while.15 = (s32[]{:T(128)}, f32[1024]{0:T(1024)S(1)}, f32[1024]{0:T(1024)S(1)}, s32[1024]{0:T(1024)S(1)}, s32[8]{0:T(128)S(1)}, /*index=5*/s32[]{:T(128)}, bf16...) while((s32[]{:T(128)}, f32[1024]{0:T(1024)S(1)}, ...), condition=%wide.region_5.6_spmd.clone, body=%wide.region_2.5_spmd.clone.sunk | while | flops 540543488 | bytes 1614283 | solution.py:77
  119.1 2.5 %fusion.18 = (f32[1024]{0:T(1024)S(1)}, f32[1024]{0:T(1024)S(1)}) fusion(s32[1024]{0:T(1024)S(1)} %get-tuple-element.256, s32[512]{0:T(512)S(1)} %iota_add_fusion.2, bf16[1024,512]{1,0:T(8,128)(2,1)} %get-tuple-element.260, bf16[4096,512]{1,0:T(8,128)(2,1)} %get-tuple-element.259, s32[]{:T(128)S(6)} %select_n.71), kind=kOutput, calls=%fused_computation.3.clone.1 | convolution fusion | flops 540538880 | bytes 1587204 | tf_op jit(solution)/shard_map/while/body/eval_jaxpr/nd,cd->nc/dot_general | solution.py:30
  122.9 2.4 %fusion.18 = (f32[1024]{0:T(1024)S(1)}, f32[1024]{0:T(1024)S(1)}) fusion(s32[1024]{0:T(1024)S(1)} %get-tuple-element.256, s32[512]{0:T(512)S(1)} %iota_add_fusion.2, bf16[1024,512]{1,0:T(8,128)(2,1)} %get-tuple-element.260, bf16[4096,512]{1,0:T(8,128)(2,1)} %get-tuple-element.259, s32[]{:T(128)S(6)} %select_n.71), kind=kOutput, calls=%fused_computation.3.clone.1 | convolution fusion | flops 540538880 | bytes 1587204 | tf_op jit(solution)/shard_map/while/body/eval_jaxpr/nd,cd->nc/dot_general | solution.py:30
  126.8 2.5 %fusion.18 = (f32[1024]{0:T(1024)S(1)}, f32[1024]{0:T(1024)S(1)}) fusion(s32[1024]{0:T(1024)S(1)} %get-tuple-element.256, s32[512]{0:T(512)S(1)} %iota_add_fusion.2, bf16[1024,512]{1,0:T(8,128)(2,1)} %get-tuple-element.260, bf16[4096,512]{1,0:T(8,128)(2,1)} %get-tuple-element.259, s32[]{:T(128)S(6)} %select_n.71), kind=kOutput, calls=%fused_computation.3.clone.1 | convolution fusion | flops 540538880 | bytes 1587204 | tf_op jit(solution)/shard_map/while/body/eval_jaxpr/nd,cd->nc/dot_general | solution.py:30
  130.6 2.4 %fusion.18 = (f32[1024]{0:T(1024)S(1)}, f32[1024]{0:T(1024)S(1)}) fusion(s32[1024]{0:T(1024)S(1)} %get-tuple-element.256, s32[512]{0:T(512)S(1)} %iota_add_fusion.2, bf16[1024,512]{1,0:T(8,128)(2,1)} %get-tuple-element.260, bf16[4096,512]{1,0:T(8,128)(2,1)} %get-tuple-element.259, s32[]{:T(128)S(6)} %select_n.71), kind=kOutput, calls=%fused_computation.3.clone.1 | convolution fusion | flops 540538880 | bytes 1587204 | tf_op jit(solution)/shard_map/while/body/eval_jaxpr/nd,cd->nc/dot_general | solution.py:30
  134.5 2.5 %fusion.18 = (f32[1024]{0:T(1024)S(1)}, f32[1024]{0:T(1024)S(1)}) fusion(s32[1024]{0:T(1024)S(1)} %get-tuple-element.256, s32[512]{0:T(512)S(1)} %iota_add_fusion.2, bf16[1024,512]{1,0:T(8,128)(2,1)} %get-tuple-element.260, bf16[4096,512]{1,0:T(8,128)(2,1)} %get-tuple-element.259, s32[]{:T(128)S(6)} %select_n.71), kind=kOutput, calls=%fused_computation.3.clone.1 | convolution fusion | flops 540538880 | bytes 1587204 | tf_op jit(solution)/shard_map/while/body/eval_jaxpr/nd,cd->nc/dot_general | solution.py:30
  138.3 2.4 %fusion.18 = (f32[1024]{0:T(1024)S(1)}, f32[1024]{0:T(1024)S(1)}) fusion(s32[1024]{0:T(1024)S(1)} %get-tuple-element.256, s32[512]{0:T(512)S(1)} %iota_add_fusion.2, bf16[1024,512]{1,0:T(8,128)(2,1)} %get-tuple-element.260, bf16[4096,512]{1,0:T(8,128)(2,1)} %get-tuple-element.259, s32[]{:T(128)S(6)} %select_n.71), kind=kOutput, calls=%fused_computation.3.clone.1 | convolution fusion | flops 540538880 | bytes 1587204 | tf_op jit(solution)/shard_map/while/body/eval_jaxpr/nd,cd->nc/dot_general | solution.py:30
  142.1 2.5 %fusion.18 = (f32[1024]{0:T(1024)S(1)}, f32[1024]{0:T(1024)S(1)}) fusion(s32[1024]{0:T(1024)S(1)} %get-tuple-element.256, s32[512]{0:T(512)S(1)} %iota_add_fusion.2, bf16[1024,512]{1,0:T(8,128)(2,1)} %get-tuple-element.260, bf16[4096,512]{1,0:T(8,128)(2,1)} %get-tuple-element.259, s32[]{:T(128)S(6)} %select_n.71), kind=kOutput, calls=%fused_computation.3.clone.1 | convolution fusion | flops 540538880 | bytes 1587204 | tf_op jit(solution)/shard_map/while/body/eval_jaxpr/nd,cd->nc/dot_general | solution.py:30
  146.0 2.4 %fusion.18 = (f32[1024]{0:T(1024)S(1)}, f32[1024]{0:T(1024)S(1)}) fusion(s32[1024]{0:T(1024)S(1)} %get-tuple-element.256, s32[512]{0:T(512)S(1)} %iota_add_fusion.2, bf16[1024,512]{1,0:T(8,128)(2,1)} %get-tuple-element.260, bf16[4096,512]{1,0:T(8,128)(2,1)} %get-tuple-element.259, s32[]{:T(128)S(6)} %select_n.71), kind=kOutput, calls=%fused_computation.3.clone.1 | convolution fusion | flops 540538880 | bytes 1587204 | tf_op jit(solution)/shard_map/while/body/eval_jaxpr/nd,cd->nc/dot_general | solution.py:30
  148.5 6.0 %all-reduce.2 = (f32[1024]{0:T(1024)S(1)}, f32[1024]{0:T(1024)S(1)}) all-reduce(f32[1024]{0:T(1024)S(1)} %get-tuple-element.111, f32[1024]{0:T(1024)S(1)} %get-tuple-element.112), channel_id=2, replica_groups=mesh['blk'=8,'dp'=4] {'dp'}, use_global_device_ids=true, to_apply=%region_6.7.clone | all-reduce | flops 2048 | bytes 16384
  (58 shorter events, 12.8 us)
Async XLA Ops:
  6.5 105.6 %copy-start = (bf16[512,512]{1,0:T(8,128)(2,1)S(1)}, bf16[512,512]{1,0:T(8,128)(2,1)}, u32[]{:S(2)}) copy-start(bf16[512,512]{1,0:T(8,128)(2,1)} %param.6) | copy-start | bytes 1572868
  6.5 111.2 %all-gather.3.cloned.1.call-start = ((), (), s32[]{:S(2)}) async-start(), calls=%async_computation | async-start | bytes 1310720 | tf_op jit(solution)/shard_map/all_gather | solution.py:60
  9.1 18.0 %collective-permute-start = (bf16[512,512]{1,0:T(8,128)(2,1)S(1)}, bf16[512,512]{1,0:T(8,128)(2,1)S(1)}, u32[]{:S(2)}, u32[]{:S(2)}) collective-permute-start(bf16[512,512]{1,0:T(8,128)(2,1)S(1)} %fusion.8), channel_id=1, source_target_pairs={{0,4},{4,8},{8,12},{12,16},{16,20},{20,24},{24,28},{28,0},{1,5},{5... | collective-permute-start | bytes 1572872 | tf_op jit(solution)/shard_map/ppermute | solution.py:49
  27.0 15.8 %collective-permute-start.1 = (bf16[512,512]{1,0:T(8,128)(2,1)S(1)}, bf16[512,512]{1,0:T(8,128)(2,1)S(1)}, u32[]{:S(2)}, u32[]{:S(2)}) collective-permute-start(bf16[512,512]{1,0:T(8,128)(2,1)S(1)} %collective-permute-done), channel_id=1, source_target_pairs={{0,4},{4,8},{8,12},{12,16},{16,20},{20,24},{24,28},{28,0},{1,5},{5... | collective-permute-start | bytes 1572872 | tf_op jit(solution)/shard_map/ppermute | solution.py:49
  42.8 14.9 %collective-permute-start.2 = (bf16[512,512]{1,0:T(8,128)(2,1)S(1)}, bf16[512,512]{1,0:T(8,128)(2,1)S(1)}, u32[]{:S(2)}, u32[]{:S(2)}) collective-permute-start(bf16[512,512]{1,0:T(8,128)(2,1)S(1)} %collective-permute-done.1), channel_id=1, source_target_pairs={{0,4},{4,8},{8,12},{12,16},{16,20},{20,24},{24,28},{28,0},{1,5},{5... | collective-permute-start | bytes 1572872 | tf_op jit(solution)/shard_map/ppermute | solution.py:49
  57.7 14.1 %collective-permute-start.3 = (bf16[512,512]{1,0:T(8,128)(2,1)S(1)}, bf16[512,512]{1,0:T(8,128)(2,1)S(1)}, u32[]{:S(2)}, u32[]{:S(2)}) collective-permute-start(bf16[512,512]{1,0:T(8,128)(2,1)S(1)} %collective-permute-done.2), channel_id=1, source_target_pairs={{0,4},{4,8},{8,12},{12,16},{16,20},{20,24},{24,28},{28,0},{1,5},{5... | collective-permute-start | bytes 1572872 | tf_op jit(solution)/shard_map/ppermute | solution.py:49
  71.8 13.2 %collective-permute-start.4 = (bf16[512,512]{1,0:T(8,128)(2,1)S(1)}, bf16[512,512]{1,0:T(8,128)(2,1)S(1)}, u32[]{:S(2)}, u32[]{:S(2)}) collective-permute-start(bf16[512,512]{1,0:T(8,128)(2,1)S(1)} %collective-permute-done.3), channel_id=1, source_target_pairs={{0,4},{4,8},{8,12},{12,16},{16,20},{20,24},{24,28},{28,0},{1,5},{5... | collective-permute-start | bytes 1572872 | tf_op jit(solution)/shard_map/ppermute | solution.py:49
  85.0 12.5 %collective-permute-start.5 = (bf16[512,512]{1,0:T(8,128)(2,1)S(1)}, bf16[512,512]{1,0:T(8,128)(2,1)}, u32[]{:S(2)}, u32[]{:S(2)}) collective-permute-start(bf16[512,512]{1,0:T(8,128)(2,1)S(1)} %collective-permute-done.4), channel_id=1, source_target_pairs={{0,4},{4,8},{8,12},{12,16},{16,20},{20,24},{24,28},{28,0},{1,5},{5... | collective-permute-start | bytes 1572872 | tf_op jit(solution)/shard_map/ppermute | solution.py:49
  97.5 12.2 %collective-permute-start.6 = (bf16[512,512]{1,0:T(8,128)(2,1)}, bf16[512,512]{1,0:T(8,128)(2,1)}, u32[]{:S(2)}, u32[]{:S(2)}) collective-permute-start(bf16[512,512]{1,0:T(8,128)(2,1)} %collective-permute-done.5), channel_id=1, source_target_pairs={{0,4},{4,8},{8,12},{12,16},{16,20},{20,24},{24,28},{28,0},{1,5},{5... | collective-permute-start | bytes 1572872 | tf_op jit(solution)/shard_map/ppermute | solution.py:49
Sparse Core Ops, SparseCore 0:
  100.5 17.1 all-gather.2
